TPU v7x, 32 devices: a whole 2x2x4 slice. The times are simulated.
32 devices in a mesh: dp: 4 (over y, core), expert: 4 (over z), pipe: 2 (over x).
Axes of the slice: x: 2, y: 2, z: 4, core: 2. Of those that a mesh axis runs over, the one named last changes fastest.
Arguments:
- inputs: bfloat16 [512, 4096], P('expert'), may hold values from -6 to 6
- cotangents: bfloat16 [512, 4096], P('expert'), may hold values from -6 to 6
- routes: int32 [512, 2], P('expert'), may hold values from 0 to 3, all different within a row; in each aligned block of 128 rows (0 to 127, 128 to 255, ...) at most 128 rows name the same one
- gates: float32 [512, 2], P('expert'), may hold values from 0.1 to 1
- w_gate: bfloat16 [4, 4096, 7168], P('expert', None, ('dp', 'pipe')), may hold values from -0.09375 to 0.09375
- w_up: bfloat16 [4, 4096, 7168], P('expert', None, ('dp', 'pipe')), may hold values from -0.09375 to 0.09375
- w_down: bfloat16 [4, 7168, 4096], P('expert', ('dp', 'pipe')), may hold values from -0.09375 to 0.09375
- proj_in: bfloat16 [4096, 32], replicated, may hold values from -0.09375 to 0.09375
- proj_out: bfloat16 [4096, 64], replicated, may hold values from -0.09375 to 0.09375
- proj_hid_a: bfloat16 [7168, 32], P(('dp', 'pipe')), may hold values from -0.0625 to 0.0625
- proj_hid_b: bfloat16 [7168, 64], P(('dp', 'pipe')), may hold values from -0.0625 to 0.0625
- queries: bfloat16 [256, 6144], P(('dp', 'pipe')), may hold values from -0.078125 to 0.078125
Outputs:
- token_scores: float32 [512, 256], P('expert', ('dp', 'pipe'))
- query_totals: float32 [256], P(('dp', 'pipe'))
Inputs may be any that keep to these rules, and one draw needn't show every extreme that they name: `routes`: each row names two different experts. Among the 128 tokens of one index of expert (aligned blocks), no expert is named more than 128 times, and in some blocks one expert is named exactly 128 times.
All inputs are finite; a program needn't handle non-finite values.
Results may differ from a plain program's by a relative error of at most 0.0041.
Values may be sent and summed in bfloat16 or wider, within the bound.
A program may use at most 128 MiB of HBM per device.

v0:
```python
import math

import jax
import jax.numpy as jnp
from jax import lax
from jax.sharding import PartitionSpec as P


def slot_matrix(route_rows, gate_rows, experts, capacity):
    count = route_rows.shape[0]
    flat = route_rows.reshape(-1)
    labels = jnp.arange(experts, dtype=jnp.int32)
    onehot = (flat[:, None] == labels[None, :]).astype(jnp.int32)
    earlier = jnp.cumsum(onehot, axis=0) - onehot
    position = jnp.sum(onehot * (labels[None, :] * capacity + earlier), axis=1)
    slot_ids = jnp.arange(experts * capacity, dtype=jnp.int32)
    table = (
        (position[None, :] == slot_ids[:, None])
        .astype(jnp.float32)
        .reshape(experts * capacity, count, 2)
    )
    picks = jnp.sum(table, axis=2)
    weighted = jnp.sum(table * gate_rows[None, :, :], axis=2)
    return (picks, weighted)


def send_back(scores):
    return lax.all_to_all(scores, "expert", split_axis=0, concat_axis=0, tiled=True)


def body(
    inputs,
    cotangents,
    routes,
    gates,
    w_gate,
    w_up,
    w_down,
    proj_in,
    proj_out,
    proj_hid_a,
    proj_hid_b,
    queries,
):
    experts = lax.axis_size("expert")
    count = inputs.shape[0]
    width = inputs.shape[1]
    capacity = 4 * count // experts
    query_count = queries.shape[0]
    gate_proj = w_gate[0]
    up_proj = w_up[0]
    down_proj = w_down[0]
    picks, weighted = slot_matrix(routes, gates, experts, capacity)
    pick_rows = picks.astype(jnp.bfloat16)
    columns = width // lax.axis_size(("dp", "pipe"))
    column_start = lax.axis_index(("dp", "pipe")) * columns
    part_in = lax.dynamic_slice_in_dim(inputs, column_start, columns, 1)
    part_back = lax.dynamic_slice_in_dim(cotangents, column_start, columns, 1)
    buffer_in = jnp.dot(pick_rows, part_in, preferred_element_type=jnp.float32).astype(jnp.bfloat16)
    buffer_back = jnp.dot(pick_rows, part_back, preferred_element_type=jnp.float32).astype(
        jnp.bfloat16
    )
    sent_in, sent_back = (
        lax.all_to_all(
            buffer_in.reshape(experts, capacity, columns),
            "expert",
            split_axis=0,
            concat_axis=0,
            tiled=True,
        ),
        lax.all_to_all(
            buffer_back.reshape(experts, capacity, columns),
            "expert",
            split_axis=0,
            concat_axis=0,
            tiled=True,
        ),
    )
    full_in, full_back = (
        lax.all_gather(sent_in, ("dp", "pipe"), axis=2, tiled=True),
        lax.all_gather(sent_back, ("dp", "pipe"), axis=2, tiled=True),
    )
    slot_in = full_in.reshape(-1, width)
    gate_pre = jnp.dot(slot_in, gate_proj, preferred_element_type=jnp.float32)
    up_pre = jnp.dot(slot_in, up_proj, preferred_element_type=jnp.float32)
    sigma = jax.nn.sigmoid(gate_pre)
    hidden = (gate_pre * sigma * up_pre).astype(jnp.bfloat16)
    a_part = jnp.dot(hidden, proj_hid_a, preferred_element_type=jnp.float32)
    slot_back = full_back.reshape(-1, width)
    gate_pre, up_pre, sigma, a_part = (gate_pre, up_pre, sigma, a_part)
    back = lax.dot_general(
        slot_back, down_proj, (((1,), (1,)), ((), ())), preferred_element_type=jnp.float32
    )
    d_up = (back * gate_pre * sigma).astype(jnp.bfloat16)
    d_gate = (back * up_pre * sigma * (1.0 + gate_pre * (1.0 - sigma))).astype(jnp.bfloat16)
    b_up_part = jnp.dot(d_up, proj_hid_b, preferred_element_type=jnp.float32)
    b_gate_part = jnp.dot(d_gate, proj_hid_b, preferred_element_type=jnp.float32)
    a_hidden, b_up, b_gate = lax.psum((a_part, b_up_part, b_gate_part), ("dp", "pipe"))
    a_input = jnp.dot(slot_in, proj_in, preferred_element_type=jnp.float32)
    b_output = jnp.dot(slot_back, proj_out, preferred_element_type=jnp.float32)
    height = slot_in.shape[0]
    sketch = jnp.concatenate(
        [
            (a_hidden[:, :, None] * b_output[:, None, :]).reshape(height, -1),
            (a_input[:, :, None] * b_up[:, None, :]).reshape(height, -1),
            (a_input[:, :, None] * b_gate[:, None, :]).reshape(height, -1),
        ],
        axis=1,
    ).astype(jnp.bfloat16)
    scores = lax.dot_general(
        sketch, queries, (((1,), (1,)), ((), ())), preferred_element_type=jnp.float32
    )
    returned = send_back(scores.reshape(experts, capacity, query_count))
    token_scores = lax.dot_general(
        weighted,
        returned.reshape(-1, query_count),
        (((0,), (0,)), ((), ())),
        precision=lax.Precision.HIGHEST,
        preferred_element_type=jnp.float32,
    )
    scale = 1.0 / math.sqrt(count * experts)
    partial_sum = jnp.sum(token_scores, axis=0)
    totals = lax.psum(partial_sum, "expert")
    return (token_scores, totals * scale)


def solution(mesh):
    placed = (
        P("expert", None),
        P("expert", None),
        P("expert", None),
        P("expert", None),
        P("expert", None, ("dp", "pipe")),
        P("expert", None, ("dp", "pipe")),
        P("expert", ("dp", "pipe"), None),
        P(),
        P(),
        P(("dp", "pipe"), None),
        P(("dp", "pipe"), None),
        P(("dp", "pipe"), None),
    )
    return jax.shard_map(
        body,
        mesh=mesh,
        in_specs=placed,
        out_specs=(P("expert", ("dp", "pipe")), P(("dp", "pipe"))),
        check_vma=False,
    )
```

profile of v0, /device:TPU:0, one launch (start us, length us, event | category | flops | bytes accessed | tf_op | source)
XLA Modules:
  0.0 218.4 jit_solution(5094420722675360818)
XLA Ops:
  7.2 0.0 copy-start
  7.2 0.0 all-gather.5.cloned.1.call-start
  7.2 0.9 copy.40
  8.1 0.1 eq.45
  8.2 0.1 eq.41
  8.4 1.2 reduce-window.6
  9.6 0.1 slice.8
  9.7 0.1 copy.42
  9.9 0.1 copy.43
  9.9 0.1 add_bitcast_fusion
  10.0 0.1 fusion.28
  10.1 0.1 eq.49
  10.3 0.1 copy.44
  10.3 0.8 convert_reduce_fusion
  11.1 0.0 copy-done
  11.2 0.3 convolution_convert_fusion
  11.5 0.0 copy-start.3
  11.5 20.9 %all_to_all.15 = bf16[4,128,512]{2,1,0:T(8,128)(2,1)} all-to-all(bf16[4,128,512]{2,1,0:T(8,128)(2,1)S(1)} %bitcast.76), channel_id=1, replica_groups=mesh['dp'=4,'expert'=4,'pipe'=2] {'expert'}, dimensions={0} | all-to-all | bytes 1048576 | tf_op jit(solution)/shard_map/all_to_all | solution.py:71
  32.3 0.0 all-gather.5.cloned.1.call-update
  32.4 0.0 all-gather.3.cloned.1.call-start
  32.4 1.2 convolution_convert_fusion.1
  33.6 16.8 %all_to_all.16 = bf16[4,128,512]{2,1,0:T(8,128)(2,1)} all-to-all(bf16[4,128,512]{2,1,0:T(8,128)(2,1)S(1)} %bitcast.75), channel_id=1, replica_groups=mesh['dp'=4,'expert'=4,'pipe'=2] {'expert'}, dimensions={0} | all-to-all | bytes 1048576 | tf_op jit(solution)/shard_map/all_to_all | solution.py:64
  50.4 0.0 all-gather.3.cloned.1.call-update
  50.4 0.0 all-reduce.3.cloned.1.call-start
  50.5 18.5 %all-gather.5.cloned.1.call-done = bf16[4,128,4096]{2,1,0:T(8,128)(2,1)} async-done(((bf16[4,128,512]{2,1,0:T(8,128)(2,1)}), bf16[4,128,4096]{2,1,0:T(8,128)(2,1)}) %all-gather.5.cloned.1.call-update) | async-done | bytes 4194320 | tf_op jit(solution)/shard_map/all_gather | solution.py:81
  69.0 0.0 copy-done.3
  69.0 0.0 copy-start.1
  69.0 3.7 %fusion.36 = f32[512,64]{0,1:T(8,128)S(1)} fusion(bf16[512,4096]{1,0:T(8,128)(2,1)} %bitcast.67, bf16[4096,64]{0,1:T(8,128)(2,1)S(1)} %copy-done.3), kind=kOutput, calls=%fused_computation.53 | convolution fusion | flops 268435456 | bytes 4849664 | tf_op jit(solution)/shard_map/dot_general | solution.py:100
  72.7 0.0 copy-done.1
  72.7 8.6 %fusion = f32[512,896]{1,0:T(8,128)S(1)} fusion(bf16[512,4096]{1,0:T(8,128)(2,1)S(1)} %bitcast.68, bf16[1,896,4096]{2,1,0:T(8,128)(2,1)} %param.18), kind=kOutput, calls=%fused_computation | convolution fusion | flops 3758096384 | bytes 13369344 | tf_op jit(solution)/shard_map/dot_general | solution.py:91
  81.3 26.9 %all-gather.3.cloned.1.call-done = bf16[4,128,4096]{2,1,0:T(8,128)(2,1)} async-done(((bf16[4,128,512]{2,1,0:T(8,128)(2,1)}), bf16[4,128,4096]{2,1,0:T(8,128)(2,1)}) %all-gather.3.cloned.1.call-update) | async-done | bytes 4194320 | tf_op jit(solution)/shard_map/all_gather | solution.py:80
  108.2 0.0 copy-start.2
  108.2 10.5 %fusion.4 = f32[512,896]{1,0:T(8,128)S(1)} fusion(bf16[512,4096]{1,0:T(8,128)(2,1)} %bitcast.69, bf16[1,4096,896]{2,1,0:T(8,128)(2,1)} %param.16), kind=kOutput, calls=%fused_computation.4 | convolution fusion | flops 3758096384 | bytes 13369344 | tf_op jit(solution)/shard_map/dot_general | solution.py:84
  118.7 0.0 copy-done.2
  118.8 0.0 copy-start.6
  118.8 8.7 %fusion.2 = f32[512,896]{1,0:T(8,128)S(1)} fusion(bf16[512,4096]{1,0:T(8,128)(2,1)S(1)} %bitcast.71, bf16[1,4096,896]{2,1,0:T(8,128)(2,1)} %param.17), kind=kOutput, calls=%fused_computation.2 | convolution fusion | flops 3758096384 | bytes 13369344 | tf_op jit(solution)/shard_map/dot_general | solution.py:85
  127.5 0.0 copy-done.6
  127.5 1.3 fusion.15
  128.8 0.0 copy-start.7
  128.8 1.5 fusion.17
  130.3 0.0 copy-done.7
  130.3 0.0 copy-start.4
  130.3 1.2 fusion.16
  131.6 0.0 all-reduce.3.cloned.1.call-update
  131.6 0.0 copy-done.4
  131.6 3.5 %fusion.37 = f32[512,32]{0,1:T(8,128)S(1)} fusion(bf16[512,4096]{1,0:T(8,128)(2,1)} %bitcast.70, bf16[4096,32]{0,1:T(8,128)(2,1)S(1)} %copy-done.4), kind=kOutput, calls=%fused_computation.54 | convolution fusion | flops 134217728 | bytes 4521984 | tf_op jit(solution)/shard_map/dot_general | solution.py:99
  135.2 51.3 %all-reduce.3.cloned.1.call-done = (f32[512,64]{0,1:T(8,128)}, f32[512,64]{0,1:T(8,128)}, f32[512,32]{0,1:T(8,128)}) async-done(((f32[512,64]{0,1:T(8,128)}, f32[512,64]{0,1:T(8,128)}, f32[512,32]{0,1:T(8,128)}), (f32[512,64]{0,1:T(8,128)}, f32[512,64]{0,1:T(8,128)}, f32[512,32]{0,1:T(8,128)})) %all-reduce.3.cloned.1.call-update) | async-done | bytes 327696 | tf_op jit(solution)/shard_map/psum | solution.py:98
  186.4 0.0 copy-start.5
  186.4 3.1 %multiply_convert_fusion.1 = (bf16[512,32,64]{0,2,1:T(8,128)(2,1)S(1)}, bf16[512,32,64]{0,2,1:T(8,128)(2,1)S(1)}, bf16[512,32,64]{0,2,1:T(8,128)(2,1)S(1)}) fusion(f32[512,64]{0,1:T(8,128)} %get-tuple-element.5, f32[512,32]{0,1:T(8,128)S(1)} %fusion.37, f32[512,64]{0,1:T(8,128)} %get-tuple-element.4, f32[512,64]{0,1:T(8,128)S(1)} %fusion.36, ...), kind=kLoop, calls=%fused_computation.13 | loop fusion | flops 6291456 | bytes 6815744 | tf_op jit(solution)/shard_map/convert.4
  189.6 0.0 copy-done.5
  189.6 1.3 fusion.12
  190.9 10.1 %all_to_all.17 = f32[4,128,32]{1,2,0:T(8,128)S(1)} all-to-all(f32[4,128,32]{1,2,0:T(8,128)S(1)} %bitcast.77), channel_id=1, replica_groups=mesh['dp'=4,'expert'=4,'pipe'=2] {'expert'}, dimensions={0} | all-to-all | bytes 131072 | tf_op jit(solution)/shard_map/all_to_all | solution.py:28
  201.1 1.0 fusion.35
  202.1 9.3 %psum.31 = f32[32]{0:T(128)S(1)} all-reduce(f32[32]{0:T(128)S(1)} %get-tuple-element.9), channel_id=1, replica_groups=mesh['dp'=4,'expert'=4,'pipe'=2] {'expert'}, use_global_device_ids=true, to_apply=%region_9.10 | all-reduce | flops 32 | bytes 256 | tf_op jit(solution)/shard_map/psum | solution.py:123
  211.3 0.5 broadcast_multiply_fusion
  (5 shorter events, 0.1 us)
Async XLA Ops:
  7.2 4.0 %copy-start = (bf16[128,4096]{1,0:T(8,128)(2,1)S(1)}, bf16[128,4096]{1,0:T(8,128)(2,1)}, u32[]{:S(2)}) copy-start(bf16[128,4096]{1,0:T(8,128)(2,1)} %param.13) | copy-start | bytes 3145732
  7.2 61.8 %all-gather.5.cloned.1.call-start = ((), (), s32[]{:S(2)}) async-start(), calls=%async_computation.4 | async-start | bytes 4718592 | tf_op jit(solution)/shard_map/all_gather | solution.py:81
  11.5 57.5 %copy-start.3 = (bf16[4096,64]{0,1:T(8,128)(2,1)S(1)}, bf16[4096,64]{0,1:T(8,128)(2,1)}, u32[]{:S(2)}) copy-start(bf16[4096,64]{0,1:T(8,128)(2,1)} %param.20) | copy-start | bytes 1572868
  32.4 75.9 %all-gather.3.cloned.1.call-start = ((), (), s32[]{:S(2)}) async-start(), calls=%async_computation.3 | async-start | bytes 4718592 | tf_op jit(solution)/shard_map/all_gather | solution.py:80
  50.4 136.0 %all-reduce.3.cloned.1.call-start = ((), (), s32[]{:S(2)}) async-start(), calls=%async_computation.5 | async-start | bytes 655360 | tf_op jit(solution)/shard_map/psum | solution.py:98
  69.0 3.7 %copy-start.1 = (bf16[4,128,4096]{2,1,0:T(8,128)(2,1)S(1)}, bf16[4,128,4096]{2,1,0:T(8,128)(2,1)}, u32[]{:S(2)}) copy-start(bf16[4,128,4096]{2,1,0:T(8,128)(2,1)} %all-gather.5.cloned.1.call-done) | copy-start | bytes 12582916
  108.2 10.5 %copy-start.2 = (bf16[4,128,4096]{2,1,0:T(8,128)(2,1)S(1)}, bf16[4,128,4096]{2,1,0:T(8,128)(2,1)}, u32[]{:S(2)}) copy-start(bf16[4,128,4096]{2,1,0:T(8,128)(2,1)} %all-gather.3.cloned.1.call-done) | copy-start | bytes 12582916
  118.8 8.8 %copy-start.6 = (bf16[896,64]{0,1:T(8,128)(2,1)S(1)}, bf16[896,64]{0,1:T(8,128)(2,1)}, u32[]{:S(2)}) copy-start(bf16[896,64]{0,1:T(8,128)(2,1)} %param.22) | copy-start | bytes 344068
  128.8 1.5 copy-start.7
  130.3 1.3 copy-start.4
  186.4 3.1 %copy-start.5 = (bf16[32,6144]{1,0:T(8,128)(2,1)S(1)}, bf16[32,6144]{1,0:T(8,128)(2,1)}, u32[]{:S(2)}) copy-start(bf16[32,6144]{1,0:T(8,128)(2,1)} %param.23) | copy-start | bytes 1179652
Sparse Core Ops, SparseCore 0:
  32.5 36.4 all-gather.4
  70.9 37.3 all-gather.2
  131.7 54.6 all-reduce.2
where the time goes:
time: 219 us; the launch traced here: 218 us
  waiting for transfers between devices  96.7 us (44%)
  blocking collectives  57.1 us (26%)
  matrix products  43 us (20%)
  between operations  13.9 us (6%)
  other arithmetic  5.9 us (3%)
    psum x1, waiting for transfers between devices, body(): lax.psum((a_part, b_up_part, b_gate_part), ('dp', 'pipe'))  51.3 us
    all_gather x1, waiting for transfers between devices, body(): lax.all_gather(sent_in, ('dp', 'pipe'), axis=2, tiled=True)  26.9 us
    all_to_all x1, blocking collectives, body(): lax.all_to_all(buffer_back.reshape(experts, capacity, columns), 'expert',...  20.9 us
    all_gather x1, waiting for transfers between devices, body(): lax.all_gather(sent_back, ('dp', 'pipe'), axis=2, tiled=True)  18.5 us
    all_to_all x1, blocking collectives, body(): lax.all_to_all(buffer_in.reshape(experts, capacity, columns), 'expert', s...  16.8 us
    dot_general x1, matrix products, body(): gate_pre = jnp.dot(slot_in, gate_proj, preferred_element_type=jnp.float32)  10.5 us
    all_to_all x1, blocking collectives, send_back(): lax.all_to_all(scores, 'expert', split_axis=0, concat_axis=0, tiled=True)  10.1 us
    psum x1, blocking collectives, body(): totals = lax.psum(partial_sum, 'expert')  9.28 us
  transfers between devices with their start and end apart: 3, of which 3 were waited for; matrix products, arithmetic and copies ran while one was open for 8% of the time, Pallas kernels for 0%

commit v1 on v0

v1 whole, which is shorter than its diff:
```python
import functools
import math

import jax
import jax.numpy as jnp
from jax import lax
from jax.experimental import pallas as pl
from jax.experimental.pallas import tpu as pltpu
from jax.sharding import PartitionSpec as P

MESH = pl.DeviceIdType.MESH
F32 = jnp.float32
BF16 = jnp.bfloat16
NT = (((1,), (1,)), ((), ()))


def slot_matrix(route_rows, gate_rows, experts, capacity):
    count = route_rows.shape[0]
    flat = route_rows.reshape(-1)
    labels = jnp.arange(experts, dtype=jnp.int32)
    onehot = (flat[:, None] == labels[None, :]).astype(jnp.int32)
    earlier = jnp.cumsum(onehot, axis=0) - onehot
    position = jnp.sum(onehot * (labels[None, :] * capacity + earlier), axis=1)
    slot_ids = jnp.arange(experts * capacity, dtype=jnp.int32)
    table = (
        (position[None, :] == slot_ids[:, None]).astype(F32).reshape(experts * capacity, count, 2)
    )
    picks = jnp.sum(table, axis=2)
    weighted = jnp.sum(table * gate_rows[None, :, :], axis=(1, 2))
    return (picks, weighted)


def mega(
    dims,
    buf_in,
    buf_back,
    weight_own,
    wg_hbm,
    wu_hbm,
    wd_hbm,
    p_in,
    p_out,
    p_a,
    p_b,
    query,
    ret_ref,
    tot_ref,
    x_in,
    x_back,
    wg,
    wu,
    wd,
    gate_s,
    up_s,
    ain_s,
    bout_s,
    part,
    land,
    red,
    wl,
    sc,
    ret,
    tsrc,
    tland,
    local_sem,
    z_send,
    z_recv,
    y_send,
    y_recv,
    x_send,
    x_recv,
    g1_send,
    g1_recv,
    g2_send,
    g2_recv,
    c_send,
    c_recv,
    w_send,
    w_recv,
    rs_send,
    rs_recv,
    ag_send,
    ag_recv,
    e_send,
    e_recv,
    t_send,
    t_recv,
):
    E, DP, NP, L, cap, ka, kb = dims
    H = DP // L
    N = DP * NP
    R = E * cap
    width = x_in.shape[1]
    cw = width // N
    hw = cw // 2
    G = 128 // ka
    rk = R // G
    dp = lax.axis_index("dp")
    me = lax.axis_index("expert")
    p = lax.axis_index("pipe")
    h = dp // L
    l = dp % L
    s = dp * NP + p

    def dev(d, e, q):
        return {"dp": d, "expert": e, "pipe": q}

    locals_ = []
    dense = buf_in.shape[0] == 1
    own = 0 if dense else me
    for i, (src, dst) in enumerate(
        (
            (buf_in.at[own], x_in.at[pl.ds(0, cap), :]),
            (buf_back.at[own], x_back.at[pl.ds(0, cap), :]),
            (weight_own.at[me], wl.at[pl.ds(0, cap), :]),
            (wg_hbm.at[0], wg),
            (wu_hbm.at[0], wu),
            (wd_hbm.at[0], wd),
        )
    ):
        c = pltpu.make_async_copy(src, dst, local_sem.at[i])
        locals_.append(c)

    barrier = pltpu.get_barrier_semaphore()

    def plane(k):
        t = lax.rem(s + k, N)
        return dev(t // NP, me, t % NP)

    for k in range(1, N):
        pl.semaphore_signal(barrier, inc=1, device_id=plane(k), device_id_type=MESH)
    for k in range(1, E):
        pl.semaphore_signal(
            barrier, inc=1, device_id=dev(dp, lax.rem(me + k, E), p), device_id_type=MESH
        )
    pl.semaphore_wait(barrier, N + E - 2)

    bufs = (buf_in, buf_back)
    xs = (x_in, x_back)

    def rc(src, dst, ss, rs, to):
        return pltpu.make_async_remote_copy(
            src_ref=src, dst_ref=dst, send_sem=ss, recv_sem=rs, device_id=to, device_id_type=MESH
        )

    def cols(share, off=0, size=None):
        size = cw if size is None else size
        return pl.ds(pl.multiple_of(share * cw + off, 128), size)

    def rows(d):
        return pl.ds(pl.multiple_of(d * cap, 8), cap)

    def share(k, kp, lane=None):
        lane = l if lane is None else lane
        return (lax.rem(h - k + H, H) * L + lane) * NP + lax.rem(p - kp + NP, NP)

    def zc(a, d):
        dst = lax.rem(me - d + E, E)
        src = bufs[a].at[0 if dense else dst, :, cols(s)]
        return rc(src, xs[a].at[rows(d), cols(s)], z_send.at[a, d - 1], z_recv.at[a, d - 1], dev(dp, dst, p))

    def yc(a, k, d):
        r = xs[a].at[rows(d), cols(s)]
        return rc(r, r, y_send.at[a, k - 1, d - 1], y_recv.at[a, k - 1, d - 1], dev(lax.rem(h + k, H) * L + l, me, p))

    def xc(a, kp, d):
        r = xs[a].at[rows(d), cols(s)]
        return rc(r, r, x_send.at[a, kp - 1, d - 1], x_recv.at[a, kp - 1, d - 1], dev(dp, me, lax.rem(p + kp, NP)))

    def g1(a, k, kp, d):
        r = xs[a].at[rows(d), cols(share(k, 0), 0, hw)]
        i = (a, k - 1, kp - 1, d - 1)
        return rc(r, r, g1_send.at[i], g1_recv.at[i], dev(dp, me, lax.rem(p + kp, NP)))

    def g2(a, k, kp, d):
        r = xs[a].at[rows(d), cols(share(0, kp), hw, hw)]
        i = (a, k - 1, kp - 1, d - 1)
        return rc(r, r, g2_send.at[i], g2_recv.at[i], dev(lax.rem(h + k, H) * L + l, me, p))

    def cc(a, k, kp, d):
        r = xs[a].at[rows(d), cols(share(k, kp))]
        i = (a, k, kp, d - 1)
        return rc(r, r, c_send.at[i], c_recv.at[i], dev(h * L + (1 - l), me, p))

    def wc(d):
        dst = lax.rem(me - d + E, E)
        return rc(weight_own.at[dst], wl.at[rows(d), :], w_send.at[d - 1], w_recv.at[d - 1], dev(dp, dst, p))

    def each(fn):
        def step(i, carry):
            fn(i + 1)
            return carry

        lax.fori_loop(0, E - 1, step, 0)

    KS = range(1, H)
    PS = range(1, NP)

    def stage_a(a):
        def f(d):
            zc(a, d).wait_recv()
            for k in KS:
                yc(a, k, d).start()
            for kp in PS:
                xc(a, kp, d).start()
            if L > 1:
                cc(a, 0, 0, d).start()

        each(f)

    def stage_b(a):
        def f(d):
            for k in KS:
                yc(a, k, d).wait_recv()
                for kp in PS:
                    g1(a, k, kp, d).start()
                if L > 1:
                    cc(a, k, 0, d).start()
            for kp in PS:
                xc(a, kp, d).wait_recv()
                for k in KS:
                    g2(a, k, kp, d).start()
                if L > 1:
                    cc(a, 0, kp, d).start()

        each(f)

    def stage_c(a):
        def f(d):
            for k in KS:
                for kp in PS:
                    g1(a, k, kp, d).wait_recv()
                    g2(a, k, kp, d).wait_recv()
                    if L > 1:
                        cc(a, k, kp, d).start()

        each(f)

    def stage_d(a):
        def f(d):
            if L > 1:
                for k in range(H):
                    for kp in range(NP):
                        cc(a, k, kp, d).wait_recv()

        each(f)

    def drain(a):
        def f(d):
            zc(a, d).wait_send()
            for k in KS:
                yc(a, k, d).wait_send()
            for kp in PS:
                xc(a, kp, d).wait_send()
            for k in KS:
                for kp in PS:
                    g1(a, k, kp, d).wait_send()
                    g2(a, k, kp, d).wait_send()
            if L > 1:
                for k in range(H):
                    for kp in range(NP):
                        cc(a, k, kp, d).wait_send()

        each(f)

    each(lambda d: zc(0, d).start())
    each(lambda d: zc(1, d).start())
    for c in locals_:
        c.start()
    each(lambda d: wc(d).start())
    stage_a(0)
    stage_b(0)
    stage_a(1)
    stage_c(0)
    stage_d(0)
    for i in (0, 3, 4):
        locals_[i].wait()

    MT = min(256, R)
    T = R // MT
    lane = lax.broadcasted_iota(jnp.int32, (MT, 128), 1)
    part[pl.ds(R, rk), :] = jnp.zeros((rk, 128), F32)

    def gate_up(m):
        rr = pl.ds(pl.multiple_of(m * MT, MT), MT)
        x = x_in[rr, :]
        g = jnp.dot(x, wg[...], preferred_element_type=F32)
        gate_s[rr, :] = g
        u = jnp.dot(x, wu[...], preferred_element_type=F32)
        up_s[rr, :] = u
        ain_s[rr, :] = jnp.dot(x, p_in[...], preferred_element_type=F32)

    def factor_a(m):
        rr = pl.ds(pl.multiple_of(m * MT, MT), MT)
        g = gate_s[rr, :]
        u = up_s[rr, :]
        sg = jax.nn.sigmoid(g)
        gs = g * sg
        hid = (gs * u).astype(BF16)
        gate_s[rr, :] = gs
        up_s[rr, :] = u * sg * (1.0 + g * (1.0 - sg))
        at = jnp.dot(hid, p_a[...], preferred_element_type=F32)
        for j in range(MT // rk):
            grp = m * (MT // rk) + j
            piece = at[j * rk : (j + 1) * rk, :]
            part[pl.ds(R, rk), :] += jnp.where(lane[:rk] // ka == grp, piece, 0.0)

    def down(m):
        rr = pl.ds(pl.multiple_of(m * MT, MT), MT)
        x = x_back[rr, :]
        back = lax.dot_general(x, wd[...], NT, preferred_element_type=F32)
        bout_s[rr, :] = jnp.dot(x, p_out[...], preferred_element_type=F32)
        du = (back * gate_s[rr, :]).astype(BF16)
        dg = (back * up_s[rr, :]).astype(BF16)
        bu = jnp.dot(du, p_b[...], preferred_element_type=F32)
        bg = jnp.dot(dg, p_b[...], preferred_element_type=F32)
        part[rr, :] = jnp.where(lane < kb, bu, bg)

    half = (T + 1) // 2
    pl.loop(0, half)(gate_up)
    stage_b(1)
    if T > half:
        pl.loop(half, T)(gate_up)
    stage_c(1)
    pl.loop(0, T)(factor_a)
    stage_d(1)
    locals_[1].wait()
    locals_[5].wait()
    pl.loop(0, T)(down)

    ch = (R + rk) // N

    def chunk(i):
        return pl.ds(pl.multiple_of(i * ch, 8), ch)

    def rsc(k):
        t = lax.rem(s + k, N)
        return rc(part.at[chunk(t), :], land.at[k - 1], rs_send.at[k - 1], rs_recv.at[k - 1], plane(k))

    def agc(k):
        r = red.at[chunk(s), :]
        return rc(r, r, ag_send.at[k - 1], ag_recv.at[k - 1], plane(k))

    for k in range(1, N):
        rsc(k).start()
    for k in range(1, N):
        rsc(k).wait_recv()
    total = part[chunk(s), :]
    for k in range(1, N):
        total = total + land[k - 1]
    red[chunk(s), :] = total
    for k in range(1, N):
        agc(k).start()
    each(lambda d: wc(d).wait_recv())
    locals_[2].wait()
    for k in range(1, N):
        t = lax.rem(s - k + N, N)
        r = red.at[chunk(t), :]
        rc(r, r, ag_send.at[k - 1], ag_recv.at[k - 1], plane(k)).wait_recv()

    seg = ka * kb
    lane_k = lax.broadcasted_iota(jnp.int32, (rk, 128), 1)

    def split(a):
        hi = a.astype(BF16)
        return hi, (a - hi.astype(F32)).astype(BF16)

    def spread(a, first):
        depth = a.shape[1]
        row = lax.broadcasted_iota(jnp.int32, (depth, seg), 0)
        col = lax.broadcasted_iota(jnp.int32, (depth, seg), 1)
        sel = jnp.where(row - first == col // kb, 1.0, 0.0).astype(BF16)
        hi, lo = split(a)
        return jnp.dot(hi, sel, preferred_element_type=F32) + jnp.dot(
            lo, sel, preferred_element_type=F32
        )

    def score(k):
        rr = pl.ds(pl.multiple_of(k * rk, 8), rk)
        b = red[rr, :]
        br = pltpu.roll(b, kb, 1)
        bu = jnp.where(lane_k < kb, b, br)
        bg = jnp.where(lane_k < kb, br, b)
        ah = spread(red[pl.ds(R, rk), :], k * ka)
        ai = spread(ain_s[rr, :], 0)
        q = query[...]
        reps = seg // 128

        def seg_dot(a, bb, i):
            sk = jnp.concatenate(
                [(a[:, j * 128 : (j + 1) * 128] * bb).astype(BF16) for j in range(reps)], axis=1
            )
            return lax.dot_general(
                sk, q[:, i * seg : (i + 1) * seg], NT, preferred_element_type=F32
            )

        r = seg_dot(ah, bout_s[rr, :], 0) + seg_dot(ai, bu, 1) + seg_dot(ai, bg, 2)
        sc[rr, :] = r * wl[rr, :]

    pl.loop(0, G)(score)
    tsrc[...] = jnp.broadcast_to(jnp.sum(sc[...], axis=0, keepdims=True), tsrc.shape)

    def ec(d):
        return rc(sc.at[rows(d), :], ret.at[rows(d), :], e_send.at[d - 1], e_recv.at[d - 1], dev(dp, lax.rem(me + d, E), p))

    def tc(d):
        return rc(tsrc, tland.at[d], t_send.at[d - 1], t_recv.at[d - 1], dev(dp, lax.rem(me + d, E), p))

    def go(d):
        ec(d).start()
        tc(d).start()

    each(go)
    ret_ref[pl.ds(0, cap), :] = sc[pl.ds(0, cap), :]
    tot_ref[0] = tsrc[...]
    drain(0)
    drain(1)
    each(lambda d: wc(d).wait_send())
    for k in range(1, N):
        rsc(k).wait_send()
        agc(k).wait_send()

    def fin(d):
        ec(d).wait()
        tc(d).wait()

    each(fin)
    rest = pl.ds(cap, R - cap)
    ret_ref[rest, :] = ret[rest, :]
    for d in range(1, E):
        tot_ref[d] = tland[d]


def body(
    inputs,
    cotangents,
    routes,
    gates,
    w_gate,
    w_up,
    w_down,
    proj_in,
    proj_out,
    proj_hid_a,
    proj_hid_b,
    queries,
):
    E = lax.axis_size("expert")
    DP = lax.axis_size("dp")
    NP = lax.axis_size("pipe")
    N = DP * NP
    count, width = inputs.shape
    cap = 4 * count // E
    nq = queries.shape[0]
    ff = w_gate.shape[2]
    ka = proj_in.shape[1]
    kb = proj_out.shape[1]
    L = 2 if DP % 2 == 0 else 1
    H = DP // L
    R = E * cap
    rk = R * ka // 128
    dense = cap >= count
    if dense:
        cap = count
        R = E * cap
        rk = R * ka // 128
        labels = jnp.arange(E, dtype=jnp.int32)
        hit = routes[None, :, :] == labels[:, None, None]
        slot_weight = jnp.sum(jnp.where(hit, gates[None, :, :], 0.0), axis=2)
        buf_in, buf_back = inputs[None], cotangents[None]
        picks = None
    else:
        picks, slot_weight = slot_matrix(routes, gates, E, cap)
        pick_rows = picks.astype(BF16)
        buf_in, buf_back = (
            jnp.dot(pick_rows, v, preferred_element_type=F32).astype(BF16).reshape(E, cap, width)
            for v in (inputs, cotangents)
        )
    weight_own = jnp.broadcast_to(slot_weight.reshape(E, cap, 1), (E, cap, nq))
    dims = (E, DP, NP, L, cap, ka, kb)
    V = pl.BlockSpec(memory_space=pltpu.VMEM)
    A = pl.BlockSpec(memory_space=pl.ANY)
    D = pltpu.SemaphoreType.DMA
    E1 = E - 1
    h1, p1 = max(H - 1, 1), max(NP - 1, 1)
    pairs = []
    for shape in (
        (2, E1),
        (2, h1, E1),
        (2, p1, E1),
        (2, h1, p1, E1),
        (2, h1, p1, E1),
        (2, H, NP, E1),
        (E1,),
        (N - 1,),
        (N - 1,),
        (E1,),
        (E1,),
    ):
        pairs += [D(shape), D(shape)]
    ret, tot = pl.pallas_call(
        functools.partial(mega, dims),
        name="routed_scores",
        out_shape=(
            jax.ShapeDtypeStruct((R, nq), F32),
            jax.ShapeDtypeStruct((E, 8, nq), F32),
        ),
        in_specs=[A, A, A, A, A, A, V, V, V, V, V],
        out_specs=(V, V),
        scratch_shapes=[
            pltpu.VMEM((R, width), BF16),
            pltpu.VMEM((R, width), BF16),
            pltpu.VMEM((width, ff), BF16),
            pltpu.VMEM((width, ff), BF16),
            pltpu.VMEM((ff, width), BF16),
            pltpu.VMEM((R, ff), F32),
            pltpu.VMEM((R, ff), F32),
            pltpu.VMEM((R, ka), F32),
            pltpu.VMEM((R, 2 * kb), F32),
            pltpu.VMEM((R + rk, 128), F32),
            pltpu.VMEM((N - 1, (R + rk) // N, 128), F32),
            pltpu.VMEM((R + rk, 128), F32),
            pltpu.VMEM((R, nq), F32),
            pltpu.VMEM((R, nq), F32),
            pltpu.VMEM((R, nq), F32),
            pltpu.VMEM((8, nq), F32),
            pltpu.VMEM((E, 8, nq), F32),
            D((6,)),
        ]
        + pairs,
        compiler_params=pltpu.CompilerParams(
            collective_id=0, has_side_effects=True, vmem_limit_bytes=62 * 1024 * 1024
        ),
    )(
        buf_in,
        buf_back,
        weight_own,
        w_gate,
        w_up,
        w_down,
        proj_in,
        jnp.concatenate([proj_out] * 2, axis=1),
        jnp.concatenate([proj_hid_a] * (128 // ka), axis=1),
        jnp.concatenate([proj_hid_b] * 2, axis=1),
        queries,
    )
    blocks = ret.reshape(E, cap, nq)
    if dense:
        token_scores = jnp.sum(blocks, axis=0)
    else:
        order = (lax.axis_index("expert") - jnp.arange(E) + E) % E
        token_scores = lax.dot_general(
            picks,
            blocks[order].reshape(R, nq),
            (((0,), (0,)), ((), ())),
            precision=lax.Precision.HIGHEST,
            preferred_element_type=F32,
        )
    scale = 1.0 / math.sqrt(count * E)
    return (token_scores, jnp.sum(tot[:, 0, :], axis=0) * scale)


def solution(mesh):
    both = ("dp", "pipe")
    placed = (
        P("expert", None),
        P("expert", None),
        P("expert", None),
        P("expert", None),
        P("expert", None, both),
        P("expert", None, both),
        P("expert", both, None),
        P(),
        P(),
        P(both, None),
        P(both, None),
        P(both, None),
    )
    return jax.shard_map(
        body,
        mesh=mesh,
        in_specs=placed,
        out_specs=(P("expert", both), P(both)),
        check_vma=False,
    )
```

time: 219 us -> 95.8 us (0.44)
  waiting for transfers between devices: 96.7 us -> 0 us
  Pallas kernels: 0 us -> 81.6 us
  blocking collectives: 57.1 us -> 0 us
  matrix products: 43 us -> 0 us
  between operations: 13.9 us -> 0.66 us
  local copies, waits for them, and re-layouts: 1.66 us -> 7.39 us
    pallas_call x0 -> x1, Pallas kernels: none -> 81.6 us  [body(): pl.pallas_call(functools.partial(mega, dims), name='routed_scores', out_s...]
    psum x1 -> x0, waiting for transfers between devices: 51.3 us -> none  [body(): lax.psum((a_part, b_up_part, b_gate_part), ('dp', 'pipe'))]
    all_to_all x3 -> x0, blocking collectives: 47.8 us -> none  [the longest x1 20.9 us: body(): lax.all_to_all(buffer_back.reshape(experts, capacity, columns), 'expert',...]
    all_gather x2 -> x0, waiting for transfers between devices: 45.4 us -> none  [the longest x1 26.9 us: body(): lax.all_gather(sent_in, ('dp', 'pipe'), axis=2, tiled=True)]
    dot_general x12 -> x0, matrix products: 43 us -> none  [the longest x1 10.5 us: body(): gate_pre = jnp.dot(slot_in, gate_proj, preferred_element_type=jnp.float32)]
    psum x1 -> x0, blocking collectives: 9.28 us -> none  [body(): totals = lax.psum(partial_sum, 'expert')]
    unnamed x17 -> x5, local copies, waits for them, and re-layouts: 0.9 us -> 6.52 us
    another operation x3 -> x0, other arithmetic: 4.39 us -> none
  transfers between devices with their start and end apart: 3 -> 0, of which waited for: 3 -> 0; matrix products, arithmetic and copies ran while one was open for 8% -> 0% of each run, Pallas kernels for 0% -> 0%
where the time goes in v1:
time: 95.8 us; the launch traced here: 95.4 us
  Pallas kernels  81.6 us (85%)
  local copies, waits for them, and re-layouts  7.39 us (8%)
  other arithmetic  5.71 us (6%)
    pallas_call x1, Pallas kernels, body(): pl.pallas_call(functools.partial(mega, dims), name='routed_scores', out_s...  81.6 us
    unnamed x5, local copies, waits for them, and re-layouts  6.52 us

profile of v1, /device:TPU:0, one launch (start us, length us, event | category | flops | bytes accessed | tf_op | source)
XLA Modules:
  0.0 95.4 jit_solution(9882778453376877204)
XLA Ops:
  0.6 1.0 %copy.39 = bf16[896,32]{1,0:T(8,128)(2,1)S(1)} copy(bf16[896,32]{0,1:T(8,128)(2,1)} %param.21) | data formatting | bytes 114688 | tf_op args[9]
  1.6 1.1 %copy.43 = bf16[896,64]{1,0:T(8,128)(2,1)S(1)} copy(bf16[896,64]{0,1:T(8,128)(2,1)} %param.22) | data formatting | bytes 229376 | tf_op args[10]
  2.7 1.2 %pad_maximum_fusion.1 = (bf16[896,128]{1,0:T(8,128)(2,1)}, bf16[896,128]{1,0:T(8,128)(2,1)}) fusion(bf16[896,32]{1,0:T(8,128)(2,1)S(1)} %copy.39, bf16[896,64]{1,0:T(8,128)(2,1)S(1)} %copy.43), kind=kLoop, calls=%fused_computation.1 | loop fusion | flops 1376256 | bytes 630784 | tf_op jit(solution)/shard_map/concatenate | solution.py:543
  3.8 1.5 %copy.37 = bf16[4096,64]{1,0:T(8,128)(2,1)S(1)} copy(bf16[4096,64]{0,1:T(8,128)(2,1)} %param.20) | data formatting | bytes 1048576 | tf_op args[8]
  5.4 1.6 %pad_maximum_fusion.p_out = bf16[4096,128]{1,0:T(8,128)(2,1)} fusion(bf16[4096,64]{1,0:T(8,128)(2,1)S(1)} %copy.37), kind=kLoop, calls=%fused_computation | loop fusion | flops 2097152 | bytes 1572864 | tf_op jit(solution)/shard_map/concatenate | solution.py:542
  7.0 2.3 %copy.45.p_in = bf16[4096,32]{1,0:T(8,128)(2,1)} copy(bf16[4096,32]{0,1:T(8,128)(2,1)} %param.19) | data formatting | bytes 524288 | tf_op args[7]
  9.3 0.7 select_reduce_fusion
  10.0 0.9 broadcast_in_dim.30.weight_own
  10.8 81.6 %routed_scores.1 = (f32[512,32]{1,0:T(8,128)}, f32[4,8,32]{2,1,0:T(8,128)}) custom-call(bf16[1,128,4096]{2,1,0:T(8,128)(2,1)} %bitcast.3, bf16[1,128,4096]{2,1,0:T(8,128)(2,1)} %bitcast.4, f32[4,128,32]{2,1,0:T(8,128)} %broadcast_in_dim.30.weight_own, bf16[1,4096,896]{2,1,0:T(8,128)(2,1)} %wg_hbm.1, bf16[1,4096,896]{2,1,0:T(8,128)(2,1)} %wu_hbm.1, ...), custom_call_target="tpu_custom_call" | custom-call | tf_op jit(solution)/shard_map/routed_scores/pallas_call | solution.py:501
  92.5 1.0 %reduce_sum.28 = f32[128,32]{1,0:T(8,128)S(1)} reduce(f32[4,128,32]{2,1,0:T(8,128)} %bitcast.5, f32[]{:T(128)} %constant.0.clone.1), dimensions={0}, to_apply=%region_1.2 | reduce | flops 12288 | bytes 81924 | tf_op jit(solution)/shard_map/reduce_sum | solution.py:549
  93.4 0.7 copy.46
  94.1 0.7 slice_reduce_fusion
  94.9 0.5 broadcast_multiply_fusion

commit v2 on v1

--- a/solution.py
+++ b/solution.py
@@ -281,6 +281,11 @@
     lane = lax.broadcasted_iota(jnp.int32, (MT, 128), 1)
     part[pl.ds(R, rk), :] = jnp.zeros((rk, 128), F32)
 
+    def wide(v, proj, times):
+        return lax.dot_general(
+            v, jnp.concatenate([proj[...]] * times, axis=0), NT, preferred_element_type=F32
+        )
+
     def gate_up(m):
         rr = pl.ds(pl.multiple_of(m * MT, MT), MT)
         x = x_in[rr, :]
@@ -288,7 +293,7 @@
         gate_s[rr, :] = g
         u = jnp.dot(x, wu[...], preferred_element_type=F32)
         up_s[rr, :] = u
-        ain_s[rr, :] = jnp.dot(x, p_in[...], preferred_element_type=F32)
+        ain_s[rr, :] = lax.dot_general(x, p_in[...], NT, preferred_element_type=F32)
 
     def factor_a(m):
         rr = pl.ds(pl.multiple_of(m * MT, MT), MT)
@@ -299,7 +304,7 @@
         hid = (gs * u).astype(BF16)
         gate_s[rr, :] = gs
         up_s[rr, :] = u * sg * (1.0 + g * (1.0 - sg))
-        at = jnp.dot(hid, p_a[...], preferred_element_type=F32)
+        at = wide(hid, p_a, 128 // ka)
         for j in range(MT // rk):
             grp = m * (MT // rk) + j
             piece = at[j * rk : (j + 1) * rk, :]
@@ -309,11 +314,11 @@
         rr = pl.ds(pl.multiple_of(m * MT, MT), MT)
         x = x_back[rr, :]
         back = lax.dot_general(x, wd[...], NT, preferred_element_type=F32)
-        bout_s[rr, :] = jnp.dot(x, p_out[...], preferred_element_type=F32)
+        bout_s[rr, :] = wide(x, p_out, 2)
         du = (back * gate_s[rr, :]).astype(BF16)
         dg = (back * up_s[rr, :]).astype(BF16)
-        bu = jnp.dot(du, p_b[...], preferred_element_type=F32)
-        bg = jnp.dot(dg, p_b[...], preferred_element_type=F32)
+        bu = wide(du, p_b, 2)
+        bg = wide(dg, p_b, 2)
         part[rr, :] = jnp.where(lane < kb, bu, bg)
 
     half = (T + 1) // 2
@@ -538,10 +543,10 @@
         w_gate,
         w_up,
         w_down,
-        proj_in,
-        jnp.concatenate([proj_out] * 2, axis=1),
-        jnp.concatenate([proj_hid_a] * (128 // ka), axis=1),
-        jnp.concatenate([proj_hid_b] * 2, axis=1),
+        proj_in.T,
+        proj_out.T,
+        proj_hid_a.T,
+        proj_hid_b.T,
         queries,
     )
     blocks = ret.reshape(E, cap, nq)

time: 95.8 us -> 86.4 us (0.902)
  local copies, waits for them, and re-layouts: 7.39 us -> 1.51 us
  other arithmetic: 5.71 us -> 2.94 us
    unnamed x5 -> x1, local copies, waits for them, and re-layouts: 6.52 us -> 0.68 us
    concatenate x2 -> x0, other arithmetic: 2.77 us -> none  [the longest x1 1.62 us: body(): jnp.concatenate([proj_out] * 2, axis=1)]
where the time goes in v2:
time: 86.4 us; the launch traced here: 86.2 us
  Pallas kernels  81.1 us (94%)
  other arithmetic  2.94 us (3%)
  local copies, waits for them, and re-layouts  1.51 us (2%)
    pallas_call x1, Pallas kernels, body(): pl.pallas_call(functools.partial(mega, dims), name='routed_scores', out_s...  81.1 us

profile of v2, /device:TPU:0, one launch (start us, length us, event | category | flops | bytes accessed | tf_op | source)
XLA Modules:
  0.0 86.2 jit_solution(15142922222788794758)
XLA Ops:
  0.6 0.7 select_reduce_fusion
  1.3 0.8 broadcast_in_dim.30.weight_own
  2.2 81.1 %routed_scores.1 = (f32[512,32]{1,0:T(8,128)}, f32[4,8,32]{2,1,0:T(8,128)}) custom-call(bf16[1,128,4096]{2,1,0:T(8,128)(2,1)} %bitcast.7, bf16[1,128,4096]{2,1,0:T(8,128)(2,1)} %bitcast.8, f32[4,128,32]{2,1,0:T(8,128)} %broadcast_in_dim.30.weight_own, bf16[1,4096,896]{2,1,0:T(8,128)(2,1)} %wg_hbm.1, bf16[1,4096,896]{2,1,0:T(8,128)(2,1)} %wu_hbm.1, ...), custom_call_target="tpu_custom_call" | custom-call | tf_op jit(solution)/shard_map/routed_scores/pallas_call | solution.py:506
  83.2 1.0 %reduce_sum.28 = f32[128,32]{1,0:T(8,128)S(1)} reduce(f32[4,128,32]{2,1,0:T(8,128)} %bitcast.11, f32[]{:T(128)} %constant.0.clone.1), dimensions={0}, to_apply=%region_1.2 | reduce | flops 12288 | bytes 81924 | tf_op jit(solution)/shard_map/reduce_sum | solution.py:554
  84.2 0.7 copy.19
  84.9 0.7 slice_reduce_fusion
  85.6 0.5 broadcast_multiply_fusion
